TPU v7x, 32 devices: a whole 2x2x4 slice. The times are simulated.
32 devices in a mesh: ctx: 8 (over z, core), tp: 4 (over y, x).
Axes of the slice: x: 2, y: 2, z: 4, core: 2. Of those that a mesh axis runs over, the one named last changes fastest.
Arguments:
- tokens: bfloat16 [2, 4096, 8192], P(None, 'ctx', 'tp'), may hold values from -14 to 14
- norm_gain: float32 [8192], replicated, may hold values from 0.5 to 1.5
- span_order: int32 [2, 16], replicated, may hold values from 0 to 15, each once within a row
- w_query: bfloat16 [8192, 4096], P('ctx', 'tp'), may hold values from -0.10122281 to 0.10122281
- w_key: bfloat16 [8192, 1024], P('ctx', 'tp'), may hold values from -0.10122281 to 0.10122281
- value_weight: bfloat16 [8192, 1024], P('ctx', 'tp'), may hold values from -0.0625 to 0.0625
- w_out: bfloat16 [4096, 8192], P('tp', 'ctx'), may hold values from -0.75 to 0.75
Outputs:
- mixed: bfloat16 [2, 4096, 8192], P(None, 'ctx', 'tp')
Inputs may be any that keep to these rules, and one draw needn't show every extreme that they name: Each row of span_order names every one of the 2 * 8 blocks of positions once; stored block b of a sequence holds positions span_order[b] * 256 onwards, in order.
All inputs are finite; a program needn't handle non-finite values.
Results may differ from a plain program's by a relative error of at most 0.014.
Values may be sent and summed in bfloat16 or wider, within the bound.
A program may use at most 128 MiB of HBM per device.

v0:
```python
import math
import jax
import jax.numpy as jnp
from jax import lax
from jax.sharding import PartitionSpec as P

HEAD_DIM = 128
theta_base = 500000.0
norm_eps = 1e-05
masked_score = -1e30


def normalize(flat_rows, norm_gain):
    wide = flat_rows.astype(jnp.float32)
    factor = lax.rsqrt(jnp.mean(wide * wide, axis=-1, keepdims=True) + norm_eps)
    return (wide * factor * norm_gain).astype(jnp.bfloat16)


def positions_of(span_order, first, count, block_rows):
    stored = first + jnp.arange(count, dtype=jnp.int32)
    which = stored // block_rows
    slots = jnp.arange(span_order.shape[1], dtype=jnp.int32)
    picked = jnp.sum(
        jnp.where(slots[None, None, :] == which[None, :, None], span_order[:, None, :], 0), axis=2
    )
    return picked * block_rows + stored % block_rows


def apply_rotation(value_rows, token_position, head_size):
    half = head_size // 2
    freqs = jnp.exp(-(2.0 * jnp.arange(half, dtype=jnp.float32) / head_size) * math.log(theta_base))
    angle = token_position.astype(jnp.float32)[..., None] * freqs
    cosine = jnp.cos(angle)[:, :, None, :]
    sine = jnp.sin(angle)[:, :, None, :]
    front = value_rows[..., :half]
    back = value_rows[..., half:]
    return jnp.concatenate([front * cosine - back * sine, back * cosine + front * sine], axis=-1)


def per_device(tokens, norm_gain, span_order, w_query, w_key, value_weight, w_out):
    sequence_batch, rows_dev, _ = tokens.shape
    head_size = HEAD_DIM
    query_heads = w_query.shape[1] // head_size
    key_heads = w_key.shape[1] // head_size
    group_width = query_heads // key_heads
    block_rows = rows_dev // 2
    total_rows = sequence_batch * rows_dev
    factor = 1.0 / math.sqrt(head_size)
    rank = lax.axis_index("ctx")
    whole = lax.all_gather(tokens, "tp", axis=2, tiled=True)
    normed = normalize(whole.reshape(total_rows, whole.shape[2]), norm_gain)
    query_pos = positions_of(span_order, rank * rows_dev, rows_dev, block_rows)
    latest = jnp.max(query_pos, axis=1)
    stat_shape = (sequence_batch, key_heads, group_width, rows_dev)
    initial = (
        jnp.full(stat_shape, masked_score, jnp.float32),
        jnp.zeros(stat_shape, jnp.float32),
        jnp.zeros(stat_shape + (head_size,), jnp.float32),
    )
    pieces = (
        lax.all_gather(w_query, "ctx", axis=0, tiled=True),
        lax.all_gather(w_key, "ctx", axis=0, tiled=True),
        lax.all_gather(value_weight, "ctx", axis=0, tiled=True),
    )
    query_flat, flattened_key, flattened_value = tuple(
        (jnp.dot(normed, piece, preferred_element_type=jnp.float32) for piece in pieces)
    )
    turned = apply_rotation(
        query_flat.reshape(sequence_batch, rows_dev, query_heads, head_size), query_pos, head_size
    ).astype(jnp.bfloat16)
    query = turned.reshape(sequence_batch, rows_dev, key_heads, group_width, head_size).transpose(
        0, 2, 3, 1, 4
    )
    turned = apply_rotation(
        flattened_key.reshape(sequence_batch, rows_dev, key_heads, head_size), query_pos, head_size
    ).astype(jnp.bfloat16)
    own_values = flattened_value.reshape(sequence_batch, rows_dev, key_heads, head_size).astype(
        jnp.bfloat16
    )
    key_piece = lax.all_gather(turned, "ctx", axis=1, tiled=True)
    value_piece = lax.all_gather(own_values, "ctx", axis=1, tiled=True)
    count = key_piece.shape[1]
    step_rows = 512

    def one_block(index, state):
        first = index * step_rows
        key_block = lax.dynamic_slice_in_dim(key_piece, first, step_rows, 1)
        value_block = lax.dynamic_slice_in_dim(value_piece, first, step_rows, 1)
        key_pos = positions_of(span_order, first, step_rows, block_rows)

        def update(current):
            peak, total, summed = current
            scores = (
                jnp.einsum(
                    "shgqd,skhd->shgqk", query, key_block, preferred_element_type=jnp.float32
                )
                * factor
            )
            allowed = key_pos[:, None, None, None, :] <= query_pos[:, None, None, :, None]
            scores = jnp.where(allowed, scores, masked_score)
            new_peak = jnp.maximum(peak, jnp.max(scores, axis=-1))
            weights = jnp.where(allowed, jnp.exp(scores - new_peak[..., None]), 0.0)
            shrink = jnp.exp(peak - new_peak)
            total = total * shrink + jnp.sum(weights, axis=-1)
            summed = summed * shrink[..., None] + jnp.einsum(
                "shgqk,skhd->shgqd",
                weights.astype(jnp.bfloat16),
                value_block,
                preferred_element_type=jnp.float32,
            )
            return (new_peak, total, summed)

        return lax.cond(
            jnp.all(jnp.min(key_pos, axis=1) > latest), lambda kept: kept, update, state
        )

    peak, total, summed = lax.fori_loop(0, count // step_rows, one_block, initial)
    attended = (summed / total[..., None]).astype(jnp.bfloat16)
    attended = attended.transpose(0, 3, 1, 2, 4).reshape(total_rows, query_heads * head_size)
    terms = jnp.dot(
        attended,
        lax.all_gather(w_out, "ctx", axis=1, tiled=True),
        preferred_element_type=jnp.float32,
    )
    mixed = lax.psum_scatter(terms.astype(jnp.bfloat16), "tp", scatter_dimension=1, tiled=True)
    return mixed.reshape(sequence_batch, rows_dev, mixed.shape[1])


def solution(mesh):
    placed = (
        P(None, "ctx", "tp"),
        P(),
        P(),
        P("ctx", "tp"),
        P("ctx", "tp"),
        P("ctx", "tp"),
        P("tp", "ctx"),
    )
    return jax.shard_map(
        per_device, mesh=mesh, in_specs=placed, out_specs=P(None, "ctx", "tp"), check_vma=False
    )
```

profile of v0, /device:TPU:0, one launch (start us, length us, event | category | flops | bytes accessed | tf_op | source)
XLA Modules:
  0.0 862.1 jit_solution(7252307660646929625)
XLA Ops:
  10.5 48.0 %all-gather.10.cloned.1.call-done = bf16[8192,256]{1,0:T(8,128)(2,1)} async-done(((bf16[1024,256]{1,0:T(8,128)(2,1)}), bf16[8192,256]{1,0:T(8,128)(2,1)}) %all-gather.10.cloned.1.call-update) | async-done | bytes 4194320 | tf_op jit(solution)/shard_map/all_gather | solution.py:62
  58.6 6.3 copy.24
  64.9 151.7 %all-gather.8.cloned.1.call-done = bf16[2,512,8192]{2,1,0:T(8,128)(2,1)} async-done(((bf16[2,512,2048]{2,1,0:T(8,128)(2,1)}), bf16[2,512,8192]{2,1,0:T(8,128)(2,1)}) %all-gather.8.cloned.1.call-update) | async-done | bytes 16777232 | tf_op jit(solution)/shard_map/all_gather | solution.py:50
  216.5 7.5 fusion.21
  224.0 9.0 %fusion.29 = f32[2,512,2,128]{1,3,2,0:T(8,128)S(1)} fusion(bf16[2,128,8192,1]{2,1,0,3:T(8,128)(2,1)S(1)} %bitcast.69, bf16[2,512,8192]{2,1,0:T(8,128)(2,1)} %all-gather.8.cloned.1.call-done, f32[8192]{0:T(1024)S(1)} %copy-done.2, f32[2,512]{1,0:T(2,128)S(1)} %add_rsqrt_fusion), kind=kOutput, calls=%fused_computation.49 | convolution fusion | flops 4328521728 | bytes 22056960 | tf_op jit(solution)/shard_map/dot_general | solution.py:66
  234.2 30.9 %all-gather.16.cloned.1.call-done = bf16[8192,256]{1,0:T(8,128)(2,1)} async-done(((bf16[1024,256]{1,0:T(8,128)(2,1)}), bf16[8192,256]{1,0:T(8,128)(2,1)}) %all-gather.16.cloned.1.call-update) | async-done | bytes 4194320 | tf_op jit(solution)/shard_map/all_gather | solution.py:63
  265.1 6.3 copy.28
  271.4 12.7 %convolution_convert_fusion.1 = bf16[2,512,2,128]{3,1,2,0:T(8,128)(2,1)} fusion(bf16[2,128,8192,1]{2,1,0,3:T(8,128)(2,1)} %bitcast.70, bf16[2,512,8192]{2,1,0:T(8,128)(2,1)} %all-gather.8.cloned.1.call-done, f32[8192]{0:T(1024)S(1)} %copy-done.2, f32[2,512]{1,0:T(2,128)S(1)} %add_rsqrt_fusion), kind=kOutput, calls=%fused_computation.47 | convolution fusion | flops 4328783872 | bytes 21532672 | tf_op jit(solution)/shard_map/dot_general | solution.py:66
  285.2 131.2 %all-gather.14.cloned.1.call-done = bf16[8192,1024]{1,0:T(8,128)(2,1)} async-done(((bf16[1024,1024]{1,0:T(8,128)(2,1)}), bf16[8192,1024]{1,0:T(8,128)(2,1)}) %all-gather.14.cloned.1.call-update) | async-done | bytes 16777232 | tf_op jit(solution)/shard_map/all_gather | solution.py:61
  416.4 21.4 %copy.25 = bf16[1024,8192]{1,0:T(8,128)(2,1)} copy(bf16[1024,8192]{0,1:T(8,128)(2,1)} %bitcast.63) | data formatting | bytes 33554432 | tf_op jit(solution)/shard_map/dot_general | solution.py:66
  437.9 22.4 %fusion.27 = f32[2,512,8,128]{1,3,2,0:T(8,128)S(1)} fusion(bf16[8,128,8192,1]{2,1,0,3:T(8,128)(2,1)} %bitcast.64, bf16[2,512,8192]{2,1,0:T(8,128)(2,1)} %all-gather.8.cloned.1.call-done, f32[8192]{0:T(1024)S(1)} %copy-done.2, f32[2,512]{1,0:T(2,128)S(1)} %add_rsqrt_fusion), kind=kOutput, calls=%fused_computation.48 | convolution fusion | flops 17213423616 | bytes 37785600 | tf_op jit(solution)/shard_map/dot_general | solution.py:66
  469.9 6.4 copy.29
  476.3 33.8 %all-gather.18.cloned.1.call-done = bf16[2,4096,2,128]{3,1,2,0:T(8,128)(2,1)} async-done(((bf16[2,512,2,128]{3,1,2,0:T(8,128)(2,1)}), bf16[2,4096,2,128]{3,1,2,0:T(8,128)(2,1)}) %all-gather.18.cloned.1.call-update) | async-done | bytes 4194320 | tf_op jit(solution)/shard_map/all_gather | solution.py:81
  512.6 156.1 %while.19 = (s32[]{:T(128)}, f32[2,2,4,512]{3,2,1,0:T(4,128)S(1)}, f32[2,2,4,512]{3,2,1,0:T(4,128)S(1)}, f32[2,2,4,512,128]{4,3,2,1,0:T(8,128)}, s32[2,16]{1,0:T...) while((s32[]{:T(128)}, f32[2,2,4,512]{3,2,1,0:T(4,128)S(1)}, ...), condition=%wide.region_11.12_spmd, body=%wide.region_3.11_spmd.sunk | while | flops 2204700672 | bytes 64532936 | solution.py:117
  514.2 17.9 %conditional.2 = (f32[2,2,4,512]{3,2,1,0:T(4,128)S(1)}, f32[2,2,4,512]{3,2,1,0:T(4,128)S(1)}, f32[2,2,4,512,128]{4,3,2,1,0:T(8,128)}) conditional(s32[]{:T(128)} %convert_element_type.85, (s32[2,512]{1,0:T(2,128)S(1)}, s32[2,512]{1,0:T(2,128)S(1)}, s32[]{:T(128)}, bf16[2,4096,2,128]{3,1,2,0:T(8,128)(2,1)}, bf16[2,2,4,512,128]{4,3,2,1,0:T(8,128)(2,1)}, ...), branch_computations={%region_7.9_spmd, %region_10.10_spmd} | conditional | flops 2204647424 | bytes 64430148 | solution.py:113
  514.6 4.7 fusion
  519.3 4.1 fusion.2
  523.5 8.7 %multiply_add_fusion = f32[2,2,4,512,128]{4,3,2,1,0:T(8,128)} fusion(f32[2,2,4,512,128]{4,3,2,1,0:T(8,128)} %get-tuple-element.360, f32[2,2,4,512]{3,2,1,0:T(4,128)S(1)} %bitcast.76, f32[2,2,512,4,512]{4,2,3,1,0:T(8,128)S(1)} %get-tuple-element.437, f32[2,2,4,512]{3,2,1,0:T(4,128)S(1)} %max.5, pred[2,512,512]{1,2,0:T(8,128)(4,1)S(1)} %broadcast_compare_fusion, ...), kind=kOutput, calls=%fused_computation.7 | convolution fusion | flops 1096810496 | bytes 26279940 | tf_op jit(solution)/shard_map/while/body/eval_jaxpr/cond/branch_0_fun/shgqk,skhd->shgqd/dot_general | solution.py:105
  533.8 17.9 %conditional.2 = (f32[2,2,4,512]{3,2,1,0:T(4,128)S(1)}, f32[2,2,4,512]{3,2,1,0:T(4,128)S(1)}, f32[2,2,4,512,128]{4,3,2,1,0:T(8,128)}) conditional(s32[]{:T(128)} %convert_element_type.85, (s32[2,512]{1,0:T(2,128)S(1)}, s32[2,512]{1,0:T(2,128)S(1)}, s32[]{:T(128)}, bf16[2,4096,2,128]{3,1,2,0:T(8,128)(2,1)}, bf16[2,2,4,512,128]{4,3,2,1,0:T(8,128)(2,1)}, ...), branch_computations={%region_7.9_spmd, %region_10.10_spmd} | conditional | flops 2204647424 | bytes 64430148 | solution.py:113
  534.2 4.7 fusion
  538.9 4.1 fusion.2
  543.0 8.7 %multiply_add_fusion = f32[2,2,4,512,128]{4,3,2,1,0:T(8,128)} fusion(f32[2,2,4,512,128]{4,3,2,1,0:T(8,128)} %get-tuple-element.360, f32[2,2,4,512]{3,2,1,0:T(4,128)S(1)} %bitcast.76, f32[2,2,512,4,512]{4,2,3,1,0:T(8,128)S(1)} %get-tuple-element.437, f32[2,2,4,512]{3,2,1,0:T(4,128)S(1)} %max.5, pred[2,512,512]{1,2,0:T(8,128)(4,1)S(1)} %broadcast_compare_fusion, ...), kind=kOutput, calls=%fused_computation.7 | convolution fusion | flops 1096810496 | bytes 26279940 | tf_op jit(solution)/shard_map/while/body/eval_jaxpr/cond/branch_0_fun/shgqk,skhd->shgqd/dot_general | solution.py:105
  553.3 17.9 %conditional.2 = (f32[2,2,4,512]{3,2,1,0:T(4,128)S(1)}, f32[2,2,4,512]{3,2,1,0:T(4,128)S(1)}, f32[2,2,4,512,128]{4,3,2,1,0:T(8,128)}) conditional(s32[]{:T(128)} %convert_element_type.85, (s32[2,512]{1,0:T(2,128)S(1)}, s32[2,512]{1,0:T(2,128)S(1)}, s32[]{:T(128)}, bf16[2,4096,2,128]{3,1,2,0:T(8,128)(2,1)}, bf16[2,2,4,512,128]{4,3,2,1,0:T(8,128)(2,1)}, ...), branch_computations={%region_7.9_spmd, %region_10.10_spmd} | conditional | flops 2204647424 | bytes 64430148 | solution.py:113
  553.7 4.7 fusion
  558.4 4.1 fusion.2
  562.5 8.7 %multiply_add_fusion = f32[2,2,4,512,128]{4,3,2,1,0:T(8,128)} fusion(f32[2,2,4,512,128]{4,3,2,1,0:T(8,128)} %get-tuple-element.360, f32[2,2,4,512]{3,2,1,0:T(4,128)S(1)} %bitcast.76, f32[2,2,512,4,512]{4,2,3,1,0:T(8,128)S(1)} %get-tuple-element.437, f32[2,2,4,512]{3,2,1,0:T(4,128)S(1)} %max.5, pred[2,512,512]{1,2,0:T(8,128)(4,1)S(1)} %broadcast_compare_fusion, ...), kind=kOutput, calls=%fused_computation.7 | convolution fusion | flops 1096810496 | bytes 26279940 | tf_op jit(solution)/shard_map/while/body/eval_jaxpr/cond/branch_0_fun/shgqk,skhd->shgqd/dot_general | solution.py:105
  572.8 17.9 %conditional.2 = (f32[2,2,4,512]{3,2,1,0:T(4,128)S(1)}, f32[2,2,4,512]{3,2,1,0:T(4,128)S(1)}, f32[2,2,4,512,128]{4,3,2,1,0:T(8,128)}) conditional(s32[]{:T(128)} %convert_element_type.85, (s32[2,512]{1,0:T(2,128)S(1)}, s32[2,512]{1,0:T(2,128)S(1)}, s32[]{:T(128)}, bf16[2,4096,2,128]{3,1,2,0:T(8,128)(2,1)}, bf16[2,2,4,512,128]{4,3,2,1,0:T(8,128)(2,1)}, ...), branch_computations={%region_7.9_spmd, %region_10.10_spmd} | conditional | flops 2204647424 | bytes 64430148 | solution.py:113
  573.2 4.7 fusion
  577.9 4.1 fusion.2
  582.0 8.7 %multiply_add_fusion = f32[2,2,4,512,128]{4,3,2,1,0:T(8,128)} fusion(f32[2,2,4,512,128]{4,3,2,1,0:T(8,128)} %get-tuple-element.360, f32[2,2,4,512]{3,2,1,0:T(4,128)S(1)} %bitcast.76, f32[2,2,512,4,512]{4,2,3,1,0:T(8,128)S(1)} %get-tuple-element.437, f32[2,2,4,512]{3,2,1,0:T(4,128)S(1)} %max.5, pred[2,512,512]{1,2,0:T(8,128)(4,1)S(1)} %broadcast_compare_fusion, ...), kind=kOutput, calls=%fused_computation.7 | convolution fusion | flops 1096810496 | bytes 26279940 | tf_op jit(solution)/shard_map/while/body/eval_jaxpr/cond/branch_0_fun/shgqk,skhd->shgqd/dot_general | solution.py:105
  592.3 17.9 %conditional.2 = (f32[2,2,4,512]{3,2,1,0:T(4,128)S(1)}, f32[2,2,4,512]{3,2,1,0:T(4,128)S(1)}, f32[2,2,4,512,128]{4,3,2,1,0:T(8,128)}) conditional(s32[]{:T(128)} %convert_element_type.85, (s32[2,512]{1,0:T(2,128)S(1)}, s32[2,512]{1,0:T(2,128)S(1)}, s32[]{:T(128)}, bf16[2,4096,2,128]{3,1,2,0:T(8,128)(2,1)}, bf16[2,2,4,512,128]{4,3,2,1,0:T(8,128)(2,1)}, ...), branch_computations={%region_7.9_spmd, %region_10.10_spmd} | conditional | flops 2204647424 | bytes 64430148 | solution.py:113
  592.7 4.8 fusion
  597.5 4.1 fusion.2
  601.7 8.6 multiply_add_fusion
  611.9 17.8 %conditional.2 = (f32[2,2,4,512]{3,2,1,0:T(4,128)S(1)}, f32[2,2,4,512]{3,2,1,0:T(4,128)S(1)}, f32[2,2,4,512,128]{4,3,2,1,0:T(8,128)}) conditional(s32[]{:T(128)} %convert_element_type.85, (s32[2,512]{1,0:T(2,128)S(1)}, s32[2,512]{1,0:T(2,128)S(1)}, s32[]{:T(128)}, bf16[2,4096,2,128]{3,1,2,0:T(8,128)(2,1)}, bf16[2,2,4,512,128]{4,3,2,1,0:T(8,128)(2,1)}, ...), branch_computations={%region_7.9_spmd, %region_10.10_spmd} | conditional | flops 2204647424 | bytes 64430148 | solution.py:113
  612.3 4.7 fusion
  617.0 4.1 fusion.2
  621.1 8.6 multiply_add_fusion
  631.4 17.8 %conditional.2 = (f32[2,2,4,512]{3,2,1,0:T(4,128)S(1)}, f32[2,2,4,512]{3,2,1,0:T(4,128)S(1)}, f32[2,2,4,512,128]{4,3,2,1,0:T(8,128)}) conditional(s32[]{:T(128)} %convert_element_type.85, (s32[2,512]{1,0:T(2,128)S(1)}, s32[2,512]{1,0:T(2,128)S(1)}, s32[]{:T(128)}, bf16[2,4096,2,128]{3,1,2,0:T(8,128)(2,1)}, bf16[2,2,4,512,128]{4,3,2,1,0:T(8,128)(2,1)}, ...), branch_computations={%region_7.9_spmd, %region_10.10_spmd} | conditional | flops 2204647424 | bytes 64430148 | solution.py:113
  631.7 4.7 fusion
  636.5 4.1 fusion.2
  640.6 8.6 multiply_add_fusion
  650.8 17.9 %conditional.2 = (f32[2,2,4,512]{3,2,1,0:T(4,128)S(1)}, f32[2,2,4,512]{3,2,1,0:T(4,128)S(1)}, f32[2,2,4,512,128]{4,3,2,1,0:T(8,128)}) conditional(s32[]{:T(128)} %convert_element_type.85, (s32[2,512]{1,0:T(2,128)S(1)}, s32[2,512]{1,0:T(2,128)S(1)}, s32[]{:T(128)}, bf16[2,4096,2,128]{3,1,2,0:T(8,128)(2,1)}, bf16[2,2,4,512,128]{4,3,2,1,0:T(8,128)(2,1)}, ...), branch_computations={%region_7.9_spmd, %region_10.10_spmd} | conditional | flops 2204647424 | bytes 64430148 | solution.py:113
  651.2 4.7 fusion
  655.9 4.1 fusion.2
  660.0 8.7 %multiply_add_fusion = f32[2,2,4,512,128]{4,3,2,1,0:T(8,128)} fusion(f32[2,2,4,512,128]{4,3,2,1,0:T(8,128)} %get-tuple-element.360, f32[2,2,4,512]{3,2,1,0:T(4,128)S(1)} %bitcast.76, f32[2,2,512,4,512]{4,2,3,1,0:T(8,128)S(1)} %get-tuple-element.437, f32[2,2,4,512]{3,2,1,0:T(4,128)S(1)} %max.5, pred[2,512,512]{1,2,0:T(8,128)(4,1)S(1)} %broadcast_compare_fusion, ...), kind=kOutput, calls=%fused_computation.7 | convolution fusion | flops 1096810496 | bytes 26279940 | tf_op jit(solution)/shard_map/while/body/eval_jaxpr/cond/branch_0_fun/shgqk,skhd->shgqd/dot_general | solution.py:105
  676.1 26.4 %convolution_convert_fusion = bf16[1024,8192]{1,0:T(8,128)(2,1)} fusion(bf16[1024,1024]{1,0:T(8,128)(2,1)} %reshape.213, bf16[1024,8192]{1,0:T(8,128)(2,1)} %all-gather.20.cloned.1.call-done), kind=kOutput, calls=%fused_computation.41 | convolution fusion | flops 17188257792 | bytes 35651584 | tf_op jit(solution)/shard_map/dot_general | solution.py:120
  702.6 152.7 %reduce-scatter.2.cloned.1.call-done = bf16[1024,2048]{1,0:T(8,128)(2,1)} async-done(((bf16[1024,8192]{1,0:T(8,128)(2,1)}), bf16[1024,2048]{1,0:T(8,128)(2,1)}) %reduce-scatter.2.cloned.1.call-update) | async-done | bytes 4194320 | tf_op jit(solution)/shard_map/reduce_scatter | solution.py:125
  (116 shorter events, 36.3 us)
Async XLA Ops:
  6.5 2.9 copy-start.1
  6.5 52.0 %all-gather.10.cloned.1.call-start = ((), (), s32[]{:S(2)}) async-start(), calls=%async_computation.2 | async-start | bytes 4718592 | tf_op jit(solution)/shard_map/all_gather | solution.py:62
  7.3 209.3 %all-gather.8.cloned.1.call-start = ((), (), s32[]{:S(2)}) async-start(), calls=%async_computation.1 | async-start | bytes 20971520 | tf_op jit(solution)/shard_map/all_gather | solution.py:50
  8.0 257.0 %all-gather.16.cloned.1.call-start = ((), (), s32[]{:S(2)}) async-start(), calls=%async_computation.5 | async-start | bytes 4718592 | tf_op jit(solution)/shard_map/all_gather | solution.py:63
  8.7 407.7 %all-gather.14.cloned.1.call-start = ((), (), s32[]{:S(2)}) async-start(), calls=%async_computation.4 | async-start | bytes 18874368 | tf_op jit(solution)/shard_map/all_gather | solution.py:61
  9.3 460.5 %all-gather.12.cloned.1.call-start = ((), (), s32[]{:S(2)}) async-start(), calls=%async_computation.3 | async-start | bytes 4718592 | tf_op jit(solution)/shard_map/all_gather | solution.py:80
  64.9 159.1 %copy-start.2 = (f32[8192]{0:T(1024)S(1)}, f32[8192]{0:T(1024)}, u32[]{:S(2)}) copy-start(f32[8192]{0:T(1024)} %param.12) | copy-start | bytes 98308
  216.5 7.5 copy-start
  234.1 276.0 %all-gather.18.cloned.1.call-start = ((), (), s32[]{:S(2)}) async-start(), calls=%async_computation.6 | async-start | bytes 4718592 | tf_op jit(solution)/shard_map/all_gather | solution.py:81
  284.1 392.1 %all-gather.20.cloned.1.call-start = ((), (), s32[]{:S(2)}) async-start(), calls=%async_computation.7 | async-start | bytes 18874368 | tf_op jit(solution)/shard_map/all_gather | solution.py:122
  284.8 570.4 %reduce-scatter.2.cloned.1.call-start = ((), (), s32[]{:S(2)}) async-start(), calls=%async_computation.8 | async-start | bytes 20971520 | tf_op jit(solution)/shard_map/reduce_scatter | solution.py:125
Sparse Core Ops, SparseCore 0:
  8.9 49.5 all-gather.9
  60.4 156.0 all-gather.7
  218.1 46.8 all-gather.15
  266.5 149.8 all-gather.13
  417.9 45.0 all-gather.11
  464.4 45.6 all-gather.17
  511.7 149.8 all-gather.19
  702.7 152.5 reduce-scatter.1
where the time goes:
time: 864 us; the launch traced here: 862 us
  waiting for transfers between devices  552 us (64%)
  matrix products  177 us (20%)
  other arithmetic  62 us (7%)
  local copies, waits for them, and re-layouts  51.1 us (6%)
  between operations  13.6 us (2%)
    reduce_scatter x1, waiting for transfers between devices, per_device(): lax.psum_scatter(terms.astype(jnp.bfloat16), 'tp', scatter_dimension=1, t...  153 us
    all_gather x1, waiting for transfers between devices, per_device(): whole = lax.all_gather(tokens, 'tp', axis=2, tiled=True)  152 us
    all_gather x1, waiting for transfers between devices, per_device(): lax.all_gather(w_query, 'ctx', axis=0, tiled=True)  131 us
    dot_general x8, matrix products, update(): jnp.einsum('shgqk,skhd->shgqd', weights.astype(jnp.bfloat16), value_block...  69.1 us
    all_gather x1, waiting for transfers between devices, per_device(): lax.all_gather(w_key, 'ctx', axis=0, tiled=True)  48 us
    dot_general x3, matrix products, per_device(): jnp.dot(normed, piece, preferred_element_type=jnp.float32)  44.1 us
    dot_general x8, matrix products, update(): jnp.einsum('shgqd,skhd->shgqk', query, key_block, preferred_element_type=...  37.6 us
    dot_general x3, local copies, waits for them, and re-layouts, per_device(): jnp.dot(normed, piece, preferred_element_type=jnp.float32)  34.1 us
  transfers between devices with their start and end apart: 8, of which 6 were waited for; matrix products, arithmetic and copies ran while one was open for 31% of the time, Pallas kernels for 0%

commit v1 on v0

--- a/solution.py
+++ b/solution.py
@@ -8,6 +8,19 @@
 theta_base = 500000.0
 norm_eps = 1e-05
 masked_score = -1e30
+
+
+def collect(shard, axis, dim):
+    ways = lax.axis_size(axis)
+    up = [(d, (d + 1) % ways) for d in range(ways)]
+    down = [(d, (d - 1) % ways) for d in range(ways)]
+    earlier, later = ([shard], [shard])
+    for _ in range(ways // 2):
+        earlier.append(lax.ppermute(earlier[-1], axis, up))
+    for _ in range((ways - 1) // 2):
+        later.append(lax.ppermute(later[-1], axis, down))
+    line = jnp.concatenate([*earlier[::-1], *later[1:]], axis=dim)
+    return jnp.roll(line, (lax.axis_index(axis) - ways // 2) * shard.shape[dim], axis=dim)
 
 
 def normalize(flat_rows, norm_gain):
@@ -58,7 +71,7 @@
         jnp.zeros(stat_shape + (head_size,), jnp.float32),
     )
     pieces = (
-        lax.all_gather(w_query, "ctx", axis=0, tiled=True),
+        collect(w_query, "ctx", 0),
         lax.all_gather(w_key, "ctx", axis=0, tiled=True),
         lax.all_gather(value_weight, "ctx", axis=0, tiled=True),
     )

time: 864 us -> 1080 us (1.25)
  waiting for transfers between devices: 552 us -> 734 us
  local copies, waits for them, and re-layouts: 51.1 us -> 77.1 us
    ppermute x0 -> x7, waiting for transfers between devices: none -> 296 us  [the longest x4 289 us: collect(): earlier.append(lax.ppermute(earlier[-1], axis, up))]
    all_gather x1 -> x0, waiting for transfers between devices: 131 us -> none  [per_device(): lax.all_gather(w_query, 'ctx', axis=0, tiled=True)]
    reduce_scatter x1, waiting for transfers between devices: 153 us -> 205 us  [per_device(): lax.psum_scatter(terms.astype(jnp.bfloat16), 'tp', scatter_dimension=1, t...]
    all_gather x1, waiting for transfers between devices: 33.8 us -> 0.01 us  [per_device(): value_piece = lax.all_gather(own_values, 'ctx', axis=1, tiled=True)]
    unnamed x6 -> x39, local copies, waits for them, and re-layouts: 0.01 us -> 17.4 us
    ppermute x0 -> x7, starting transfers between devices: none -> 11 us  [the longest x3 10.7 us: collect(): later.append(lax.ppermute(later[-1], axis, down))]
    dot_general x3 -> x4, local copies, waits for them, and re-layouts: 34.1 us -> 41.1 us  [per_device(): jnp.dot(normed, piece, preferred_element_type=jnp.float32)]
  transfers between devices with their start and end apart: 8 -> 14, of which waited for: 6 -> 9; matrix products, arithmetic and copies ran while one was open for 31% -> 27% of each run, Pallas kernels for 0% -> 0%
where the time goes in v1:
time: 1080 us
  waiting for transfers between devices  734 us (68%)
  matrix products  175 us (16%)
  local copies, waits for them, and re-layouts  77.1 us (7%)
  other arithmetic  62.5 us (6%)
  between operations  13.8 us (1%)
  starting transfers between devices  11.2 us (1%)
    ppermute x4, waiting for transfers between devices, collect(): earlier.append(lax.ppermute(earlier[-1], axis, up))  289 us
    reduce_scatter x1, waiting for transfers between devices, per_device(): lax.psum_scatter(terms.astype(jnp.bfloat16), 'tp', scatter_dimension=1, t...  205 us
    all_gather x1, waiting for transfers between devices, per_device(): whole = lax.all_gather(tokens, 'tp', axis=2, tiled=True)  152 us
    dot_general x8, matrix products, update(): jnp.einsum('shgqk,skhd->shgqd', weights.astype(jnp.bfloat16), value_block...  68.8 us
    all_gather x1, waiting for transfers between devices, per_device(): lax.all_gather(w_key, 'ctx', axis=0, tiled=True)  47.9 us
    dot_general x3, matrix products, per_device(): jnp.dot(normed, piece, preferred_element_type=jnp.float32)  42.2 us
    dot_general x4, local copies, waits for them, and re-layouts, per_device(): jnp.dot(normed, piece, preferred_element_type=jnp.float32)  41.1 us
    dot_general x8, matrix products, update(): jnp.einsum('shgqd,skhd->shgqk', query, key_block, preferred_element_type=...  37.5 us
  transfers between devices with their start and end apart: 14, of which 9 were waited for; matrix products, arithmetic and copies ran while one was open for 27% of the time, Pallas kernels for 0%

profile of v1, /device:TPU:0, one launch (start us, length us, event | category | flops | bytes accessed | tf_op | source)
XLA Modules:
  0.0 1079.2 jit_solution(13919498866640632862)
XLA Ops:
  10.6 47.9 %all-gather.9.cloned.1.call-done = bf16[8192,256]{1,0:T(8,128)(2,1)} async-done(((bf16[1024,256]{1,0:T(8,128)(2,1)}), bf16[8192,256]{1,0:T(8,128)(2,1)}) %all-gather.9.cloned.1.call-update) | async-done | bytes 4194320 | tf_op jit(solution)/shard_map/all_gather | solution.py:75
  58.6 6.3 copy.24
  64.9 151.7 %all-gather.7.cloned.1.call-done = bf16[2,512,8192]{2,1,0:T(8,128)(2,1)} async-done(((bf16[2,512,2048]{2,1,0:T(8,128)(2,1)}), bf16[2,512,8192]{2,1,0:T(8,128)(2,1)}) %all-gather.7.cloned.1.call-update) | async-done | bytes 16777232 | tf_op jit(solution)/shard_map/all_gather | solution.py:63
  216.5 7.5 fusion.21
  224.0 9.0 fusion.29
  234.2 30.8 %all-gather.13.cloned.1.call-done = bf16[8192,256]{1,0:T(8,128)(2,1)} async-done(((bf16[1024,256]{1,0:T(8,128)(2,1)}), bf16[8192,256]{1,0:T(8,128)(2,1)}) %all-gather.13.cloned.1.call-update) | async-done | bytes 4194320 | tf_op jit(solution)/shard_map/all_gather | solution.py:76
  265.1 6.3 copy.28
  271.4 10.9 %convolution_convert_fusion.1 = bf16[2,512,2,128]{3,1,2,0:T(8,128)(2,1)} fusion(bf16[2,128,8192,1]{2,1,0,3:T(8,128)(2,1)} %bitcast.70, bf16[2,512,8192]{2,1,0:T(8,128)(2,1)} %all-gather.7.cloned.1.call-done, f32[8192]{0:T(1024)S(1)} %copy-done.11, f32[2,512]{1,0:T(2,128)S(1)} %add_rsqrt_fusion), kind=kOutput, calls=%fused_computation.48 | convolution fusion | flops 4328783872 | bytes 21532672 | tf_op jit(solution)/shard_map/dot_general | solution.py:79
  283.2 50.6 %collective-permute-done = bf16[1024,1024]{1,0:T(8,128)(2,1)S(1)} collective-permute-done((bf16[1024,1024]{1,0:T(8,128)(2,1)S(1)}, bf16[1024,1024]{1,0:T(8,128)(2,1)S(1)}, u32[]{:S(2)}, u32[]{:S(2)}) %collective-permute-start) | collective-permute-done | bytes 2097184 | tf_op jit(solution)/shard_map/ppermute | solution.py:19
  337.3 77.9 %collective-permute-done.1 = bf16[1024,1024]{1,0:T(8,128)(2,1)S(1)} collective-permute-done((bf16[1024,1024]{1,0:T(8,128)(2,1)S(1)}, bf16[1024,1024]{1,0:T(8,128)(2,1)S(1)}, u32[]{:S(2)}, u32[]{:S(2)}) %collective-permute-start.1) | collective-permute-done | bytes 2097184 | tf_op jit(solution)/shard_map/ppermute | solution.py:19
  418.9 90.8 %collective-permute-done.2 = bf16[1024,1024]{1,0:T(8,128)(2,1)} collective-permute-done((bf16[1024,1024]{1,0:T(8,128)(2,1)S(1)}, bf16[1024,1024]{1,0:T(8,128)(2,1)}, u32[]{:S(2)}, u32[]{:S(2)}) %collective-permute-start.2) | collective-permute-done | bytes 2097184 | tf_op jit(solution)/shard_map/ppermute | solution.py:19
  513.4 70.0 %collective-permute-done.3 = bf16[1024,1024]{1,0:T(8,128)(2,1)} collective-permute-done((bf16[1024,1024]{1,0:T(8,128)(2,1)}, bf16[1024,1024]{1,0:T(8,128)(2,1)}, u32[]{:S(2)}, u32[]{:S(2)}) %collective-permute-start.3) | collective-permute-done | bytes 2097184 | tf_op jit(solution)/shard_map/ppermute | solution.py:19
  592.9 6.9 collective-permute-done.6
  609.5 7.0 dynamic-slice_bitcast_fusion
  616.5 21.5 %copy.25 = bf16[1024,8192]{1,0:T(8,128)(2,1)} copy(bf16[1024,8192]{0,1:T(8,128)(2,1)} %dynamic-slice_bitcast_fusion) | data formatting | bytes 33554432 | tf_op jit(solution)/shard_map/dot_general | solution.py:79
  637.9 22.3 %fusion.27 = f32[2,512,8,128]{1,3,2,0:T(8,128)S(1)} fusion(bf16[8,128,8192,1]{2,1,0,3:T(8,128)(2,1)} %bitcast.64, bf16[2,512,8192]{2,1,0:T(8,128)(2,1)} %all-gather.7.cloned.1.call-done, f32[8192]{0:T(1024)S(1)} %copy-done.11, f32[2,512]{1,0:T(2,128)S(1)} %add_rsqrt_fusion), kind=kOutput, calls=%fused_computation.49 | convolution fusion | flops 17213423616 | bytes 37785600 | tf_op jit(solution)/shard_map/dot_general | solution.py:79
  665.8 4.1 maximum_bitcast_fusion
  669.9 6.3 copy.29
  678.8 155.0 %while.19 = (s32[]{:T(128)}, f32[2,2,4,512]{3,2,1,0:T(4,128)S(1)}, f32[2,2,4,512]{3,2,1,0:T(4,128)S(1)}, f32[2,2,4,512,128]{4,3,2,1,0:T(8,128)}, s32[2,16]{1,0:T...) while((s32[]{:T(128)}, f32[2,2,4,512]{3,2,1,0:T(4,128)S(1)}, ...), condition=%wide.region_11.12_spmd, body=%wide.region_3.11_spmd.sunk | while | flops 2204700672 | bytes 64532936 | solution.py:130
  680.3 17.8 %conditional.2 = (f32[2,2,4,512]{3,2,1,0:T(4,128)S(1)}, f32[2,2,4,512]{3,2,1,0:T(4,128)S(1)}, f32[2,2,4,512,128]{4,3,2,1,0:T(8,128)}) conditional(s32[]{:T(128)} %convert_element_type.85, (s32[2,512]{1,0:T(2,128)S(1)}, s32[2,512]{1,0:T(2,128)S(1)}, s32[]{:T(128)}, bf16[2,4096,2,128]{3,1,2,0:T(8,128)(2,1)}, bf16[2,2,4,512,128]{4,3,2,1,0:T(8,128)(2,1)}, ...), branch_computations={%region_7.9_spmd, %region_10.10_spmd} | conditional | flops 2204647424 | bytes 64430148 | solution.py:126
  680.7 4.7 fusion
  685.4 4.1 fusion.2
  689.6 8.6 multiply_add_fusion
  699.7 17.8 %conditional.2 = (f32[2,2,4,512]{3,2,1,0:T(4,128)S(1)}, f32[2,2,4,512]{3,2,1,0:T(4,128)S(1)}, f32[2,2,4,512,128]{4,3,2,1,0:T(8,128)}) conditional(s32[]{:T(128)} %convert_element_type.85, (s32[2,512]{1,0:T(2,128)S(1)}, s32[2,512]{1,0:T(2,128)S(1)}, s32[]{:T(128)}, bf16[2,4096,2,128]{3,1,2,0:T(8,128)(2,1)}, bf16[2,2,4,512,128]{4,3,2,1,0:T(8,128)(2,1)}, ...), branch_computations={%region_7.9_spmd, %region_10.10_spmd} | conditional | flops 2204647424 | bytes 64430148 | solution.py:126
  700.1 4.7 fusion
  708.9 8.6 multiply_add_fusion
  719.1 17.8 %conditional.2 = (f32[2,2,4,512]{3,2,1,0:T(4,128)S(1)}, f32[2,2,4,512]{3,2,1,0:T(4,128)S(1)}, f32[2,2,4,512,128]{4,3,2,1,0:T(8,128)}) conditional(s32[]{:T(128)} %convert_element_type.85, (s32[2,512]{1,0:T(2,128)S(1)}, s32[2,512]{1,0:T(2,128)S(1)}, s32[]{:T(128)}, bf16[2,4096,2,128]{3,1,2,0:T(8,128)(2,1)}, bf16[2,2,4,512,128]{4,3,2,1,0:T(8,128)(2,1)}, ...), branch_computations={%region_7.9_spmd, %region_10.10_spmd} | conditional | flops 2204647424 | bytes 64430148 | solution.py:126
  719.5 4.7 fusion
  728.3 8.6 multiply_add_fusion
  738.5 17.8 %conditional.2 = (f32[2,2,4,512]{3,2,1,0:T(4,128)S(1)}, f32[2,2,4,512]{3,2,1,0:T(4,128)S(1)}, f32[2,2,4,512,128]{4,3,2,1,0:T(8,128)}) conditional(s32[]{:T(128)} %convert_element_type.85, (s32[2,512]{1,0:T(2,128)S(1)}, s32[2,512]{1,0:T(2,128)S(1)}, s32[]{:T(128)}, bf16[2,4096,2,128]{3,1,2,0:T(8,128)(2,1)}, bf16[2,2,4,512,128]{4,3,2,1,0:T(8,128)(2,1)}, ...), branch_computations={%region_7.9_spmd, %region_10.10_spmd} | conditional | flops 2204647424 | bytes 64430148 | solution.py:126
  738.8 4.7 fusion
  743.6 4.1 fusion.2
  747.7 8.6 multiply_add_fusion
  757.8 17.8 %conditional.2 = (f32[2,2,4,512]{3,2,1,0:T(4,128)S(1)}, f32[2,2,4,512]{3,2,1,0:T(4,128)S(1)}, f32[2,2,4,512,128]{4,3,2,1,0:T(8,128)}) conditional(s32[]{:T(128)} %convert_element_type.85, (s32[2,512]{1,0:T(2,128)S(1)}, s32[2,512]{1,0:T(2,128)S(1)}, s32[]{:T(128)}, bf16[2,4096,2,128]{3,1,2,0:T(8,128)(2,1)}, bf16[2,2,4,512,128]{4,3,2,1,0:T(8,128)(2,1)}, ...), branch_computations={%region_7.9_spmd, %region_10.10_spmd} | conditional | flops 2204647424 | bytes 64430148 | solution.py:126
  758.2 4.7 fusion
  762.9 4.1 fusion.2
  767.1 8.6 multiply_add_fusion
  777.2 17.8 %conditional.2 = (f32[2,2,4,512]{3,2,1,0:T(4,128)S(1)}, f32[2,2,4,512]{3,2,1,0:T(4,128)S(1)}, f32[2,2,4,512,128]{4,3,2,1,0:T(8,128)}) conditional(s32[]{:T(128)} %convert_element_type.85, (s32[2,512]{1,0:T(2,128)S(1)}, s32[2,512]{1,0:T(2,128)S(1)}, s32[]{:T(128)}, bf16[2,4096,2,128]{3,1,2,0:T(8,128)(2,1)}, bf16[2,2,4,512,128]{4,3,2,1,0:T(8,128)(2,1)}, ...), branch_computations={%region_7.9_spmd, %region_10.10_spmd} | conditional | flops 2204647424 | bytes 64430148 | solution.py:126
  777.6 4.7 fusion
  786.4 8.6 multiply_add_fusion
  796.6 17.8 %conditional.2 = (f32[2,2,4,512]{3,2,1,0:T(4,128)S(1)}, f32[2,2,4,512]{3,2,1,0:T(4,128)S(1)}, f32[2,2,4,512,128]{4,3,2,1,0:T(8,128)}) conditional(s32[]{:T(128)} %convert_element_type.85, (s32[2,512]{1,0:T(2,128)S(1)}, s32[2,512]{1,0:T(2,128)S(1)}, s32[]{:T(128)}, bf16[2,4096,2,128]{3,1,2,0:T(8,128)(2,1)}, bf16[2,2,4,512,128]{4,3,2,1,0:T(8,128)(2,1)}, ...), branch_computations={%region_7.9_spmd, %region_10.10_spmd} | conditional | flops 2204647424 | bytes 64430148 | solution.py:126
  797.0 4.7 fusion
  805.8 8.6 multiply_add_fusion
  816.0 17.8 %conditional.2 = (f32[2,2,4,512]{3,2,1,0:T(4,128)S(1)}, f32[2,2,4,512]{3,2,1,0:T(4,128)S(1)}, f32[2,2,4,512,128]{4,3,2,1,0:T(8,128)}) conditional(s32[]{:T(128)} %convert_element_type.85, (s32[2,512]{1,0:T(2,128)S(1)}, s32[2,512]{1,0:T(2,128)S(1)}, s32[]{:T(128)}, bf16[2,4096,2,128]{3,1,2,0:T(8,128)(2,1)}, bf16[2,2,4,512,128]{4,3,2,1,0:T(8,128)(2,1)}, ...), branch_computations={%region_7.9_spmd, %region_10.10_spmd} | conditional | flops 2204647424 | bytes 64430148 | solution.py:126
  816.3 4.7 fusion
  825.2 8.6 multiply_add_fusion
  841.2 26.4 %convolution_convert_fusion = bf16[1024,8192]{1,0:T(8,128)(2,1)} fusion(bf16[1024,1024]{1,0:T(8,128)(2,1)} %reshape.213, bf16[1024,8192]{1,0:T(8,128)(2,1)} %all-gather.17.cloned.1.call-done), kind=kOutput, calls=%fused_computation.42 | convolution fusion | flops 17188257792 | bytes 35651584 | tf_op jit(solution)/shard_map/dot_general | solution.py:133
  867.6 204.7 %reduce-scatter.2.cloned.1.call-done = bf16[1024,2048]{1,0:T(8,128)(2,1)} async-done(((bf16[1024,8192]{1,0:T(8,128)(2,1)}), bf16[1024,2048]{1,0:T(8,128)(2,1)}) %reduce-scatter.2.cloned.1.call-update) | async-done | bytes 4194320 | tf_op jit(solution)/shard_map/reduce_scatter | solution.py:138
  (162 shorter events, 82.3 us)
Async XLA Ops:
  6.5 217.5 %copy-start.11 = (f32[8192]{0:T(1024)S(1)}, f32[8192]{0:T(1024)}, u32[]{:S(2)}) copy-start(f32[8192]{0:T(1024)} %param.12) | copy-start | bytes 98308
  6.5 52.0 %all-gather.9.cloned.1.call-start = ((), (), s32[]{:S(2)}) async-start(), calls=%async_computation.2 | async-start | bytes 4718592 | tf_op jit(solution)/shard_map/all_gather | solution.py:75
  7.3 209.3 %all-gather.7.cloned.1.call-start = ((), (), s32[]{:S(2)}) async-start(), calls=%async_computation.1 | async-start | bytes 20971520 | tf_op jit(solution)/shard_map/all_gather | solution.py:63
  8.0 257.0 %all-gather.13.cloned.1.call-start = ((), (), s32[]{:S(2)}) async-start(), calls=%async_computation.4 | async-start | bytes 4718592 | tf_op jit(solution)/shard_map/all_gather | solution.py:76
  8.7 661.2 %all-gather.11.cloned.1.call-start = ((), (), s32[]{:S(2)}) async-start(), calls=%async_computation.3 | async-start | bytes 4718592 | tf_op jit(solution)/shard_map/all_gather | solution.py:93
  10.6 222.4 %copy-start.8 = (f32[2,512,64]{1,2,0:T(8,128)}, f32[2,512,64]{1,2,0:T(8,128)S(1)}, u32[]{:S(2)}) copy-start(f32[2,512,64]{1,2,0:T(8,128)S(1)} %get-tuple-element.445) | copy-start | bytes 786436
  216.5 7.5 copy-start.7
  234.2 442.1 %all-gather.15.cloned.1.call-start = ((), (), s32[]{:S(2)}) async-start(), calls=%async_computation.5 | async-start | bytes 4718592 | tf_op jit(solution)/shard_map/all_gather | solution.py:94
  271.4 11.5 %copy-start = (bf16[1024,1024]{1,0:T(8,128)(2,1)S(1)}, bf16[1024,1024]{1,0:T(8,128)(2,1)}, u32[]{:S(2)}) copy-start(bf16[1024,1024]{1,0:T(8,128)(2,1)} %param.14) | copy-start | bytes 6291460
  282.3 558.9 %all-gather.17.cloned.1.call-start = ((), (), s32[]{:S(2)}) async-start(), calls=%async_computation.6 | async-start | bytes 18874368 | tf_op jit(solution)/shard_map/all_gather | solution.py:135
  282.8 789.5 %reduce-scatter.2.cloned.1.call-start = ((), (), s32[]{:S(2)}) async-start(), calls=%async_computation.7 | async-start | bytes 20971520 | tf_op jit(solution)/shard_map/reduce_scatter | solution.py:138
  282.9 50.9 %collective-permute-start = (bf16[1024,1024]{1,0:T(8,128)(2,1)S(1)}, bf16[1024,1024]{1,0:T(8,128)(2,1)S(1)}, u32[]{:S(2)}, u32[]{:S(2)}) collective-permute-start(bf16[1024,1024]{1,0:T(8,128)(2,1)S(1)} %copy-done), channel_id=1, source_target_pairs={{0,4},{4,8},{8,12},{12,16},{16,20},{20,24},{24,28},{28,0},{1,5},{5... | collective-permute-start | bytes 6291464 | tf_op jit(solution)/shard_map/ppermute | solution.py:19
  333.8 81.5 %copy-start.1 = (bf16[1024,1024]{1,0:T(8,128)(2,1)}, bf16[1024,1024]{1,0:T(8,128)(2,1)S(1)}, u32[]{:S(2)}) copy-start(bf16[1024,1024]{1,0:T(8,128)(2,1)S(1)} %collective-permute-done) | copy-start | bytes 6291460
  333.8 81.5 %collective-permute-start.1 = (bf16[1024,1024]{1,0:T(8,128)(2,1)S(1)}, bf16[1024,1024]{1,0:T(8,128)(2,1)S(1)}, u32[]{:S(2)}, u32[]{:S(2)}) collective-permute-start(bf16[1024,1024]{1,0:T(8,128)(2,1)S(1)} %collective-permute-done), channel_id=1, source_target_pairs={{0,4},{4,8},{8,12},{12,16},{16,20},{20,24},{24,28},{28,0},{1,5},{5... | collective-permute-start | bytes 6291464 | tf_op jit(solution)/shard_map/ppermute | solution.py:19
  333.8 81.5 %collective-permute-start.4 = (bf16[1024,1024]{1,0:T(8,128)(2,1)S(1)}, bf16[1024,1024]{1,0:T(8,128)(2,1)S(1)}, u32[]{:S(2)}, u32[]{:S(2)}) collective-permute-start(bf16[1024,1024]{1,0:T(8,128)(2,1)S(1)} %copy-done), channel_id=1, source_target_pairs={{0,28},{4,0},{8,4},{12,8},{16,12},{20,16},{24,20},{28,24},{1,29},{... | collective-permute-start | bytes 6291464 | tf_op jit(solution)/shard_map/ppermute | solution.py:21
  415.3 94.4 %copy-start.5 = (bf16[1024,1024]{1,0:T(8,128)(2,1)}, bf16[1024,1024]{1,0:T(8,128)(2,1)S(1)}, u32[]{:S(2)}) copy-start(bf16[1024,1024]{1,0:T(8,128)(2,1)S(1)} %collective-permute-done.1) | copy-start | bytes 6291460
  415.3 94.4 %collective-permute-start.2 = (bf16[1024,1024]{1,0:T(8,128)(2,1)S(1)}, bf16[1024,1024]{1,0:T(8,128)(2,1)}, u32[]{:S(2)}, u32[]{:S(2)}) collective-permute-start(bf16[1024,1024]{1,0:T(8,128)(2,1)S(1)} %collective-permute-done.1), channel_id=1, source_target_pairs={{0,4},{4,8},{8,12},{12,16},{16,20},{20,24},{24,28},{28,0},{1,5},{5... | collective-permute-start | bytes 6291464 | tf_op jit(solution)/shard_map/ppermute | solution.py:19
  415.3 3.6 copy-start.3
  415.3 94.4 %collective-permute-start.5 = (bf16[1024,1024]{1,0:T(8,128)(2,1)S(1)}, bf16[1024,1024]{1,0:T(8,128)(2,1)}, u32[]{:S(2)}, u32[]{:S(2)}) collective-permute-start(bf16[1024,1024]{1,0:T(8,128)(2,1)S(1)} %collective-permute-done.4), channel_id=1, source_target_pairs={{0,28},{4,0},{8,4},{12,8},{16,12},{20,16},{24,20},{28,24},{1,29},{... | collective-permute-start | bytes 6291464 | tf_op jit(solution)/shard_map/ppermute | solution.py:21
  509.7 73.6 %collective-permute-start.3 = (bf16[1024,1024]{1,0:T(8,128)(2,1)}, bf16[1024,1024]{1,0:T(8,128)(2,1)}, u32[]{:S(2)}, u32[]{:S(2)}) collective-permute-start(bf16[1024,1024]{1,0:T(8,128)(2,1)} %collective-permute-done.2), channel_id=1, source_target_pairs={{0,4},{4,8},{8,12},{12,16},{16,20},{20,24},{24,28},{28,0},{1,5},{5... | collective-permute-start | bytes 6291464 | tf_op jit(solution)/shard_map/ppermute | solution.py:19
  509.7 90.1 %collective-permute-start.6 = (bf16[1024,1024]{1,0:T(8,128)(2,1)}, bf16[1024,1024]{1,0:T(8,128)(2,1)}, u32[]{:S(2)}, u32[]{:S(2)}) collective-permute-start(bf16[1024,1024]{1,0:T(8,128)(2,1)} %collective-permute-done.5), channel_id=1, source_target_pairs={{0,28},{4,0},{8,4},{12,8},{16,12},{20,16},{24,20},{28,24},{1,29},{... | collective-permute-start | bytes 6291464 | tf_op jit(solution)/shard_map/ppermute | solution.py:21
  513.4 77.6 %copy-start.4 = (bf16[1024,1024]{1,0:T(8,128)(2,1)S(1)}, bf16[1024,1024]{1,0:T(8,128)(2,1)}, u32[]{:S(2)}) copy-start(bf16[1024,1024]{1,0:T(8,128)(2,1)} %copy-done.3) | copy-start | bytes 6291460
  586.9 18.3 %copy-start.6 = (bf16[1024,1024]{1,0:T(8,128)(2,1)S(1)}, bf16[1024,1024]{1,0:T(8,128)(2,1)}, u32[]{:S(2)}) copy-start(bf16[1024,1024]{1,0:T(8,128)(2,1)} %copy-done.5) | copy-start | bytes 6291460
  588.9 16.5 %copy-start.2 = (bf16[1024,1024]{1,0:T(8,128)(2,1)S(1)}, bf16[1024,1024]{1,0:T(8,128)(2,1)}, u32[]{:S(2)}) copy-start(bf16[1024,1024]{1,0:T(8,128)(2,1)} %copy-done.1) | copy-start | bytes 6291460
  637.9 22.4 %copy-start.9 = (f32[2,512,64]{1,2,0:T(8,128)S(1)}, f32[2,512,64]{1,2,0:T(8,128)}, u32[]{:S(2)}) copy-start(f32[2,512,64]{1,2,0:T(8,128)} %copy-done.8) | copy-start | bytes 786436
  660.3 18.5 %copy-start.10 = (s32[2,16]{1,0:T(2,128)S(1)}, s32[2,16]{1,0:T(2,128)}, u32[]{:S(2)}) copy-start(s32[2,16]{1,0:T(2,128)} %param.13) | copy-start | bytes 388
Sparse Core Ops, SparseCore 0:
  8.9 49.5 all-gather.8
  60.4 156.0 all-gather.6
  218.1 46.8 all-gather.12
  266.5 57.1 all-gather.10
  325.1 73.0 all-gather.14
  399.7 237.5 all-gather.16
  867.8 204.5 reduce-scatter.1
